TPU v7x, 128 devices: a whole 4x4x4 slice. The times are simulated.
128 devices in a mesh: hi: 8 (over z_hi, y), lo: 16 (over z_lo, x, core).
Axes of the slice: x: 4, y: 4, z: 4 (z_hi: 2, z_lo: 2; z = z_hi * 2 + z_lo), core: 2. Of those that a mesh axis runs over, the one named last changes fastest.
Arguments:
- charges: bfloat16 [1048576, 128], P(('hi', 'lo')), may hold values from -6 to 6
- source_order: int32 [1048576], P(('hi', 'lo')), may hold values from 0 to 8191, as said below
- source_interp: bfloat16 [1048576, 128], P(('hi', 'lo')), may hold values from -0.5 to 0.5
- factors: bfloat16 [16384, 8, 128], P(('hi', 'lo')), may hold values from -6 to 6
- transfers: bfloat16 [8, 2, 2, 64, 128], replicated, may hold values from -0.375 to 0.375
- level_bits: int32 [4], replicated, may hold values from 0 to 6
- receiver_interp: bfloat16 [1048576, 128], P(('hi', 'lo')), may hold values from -0.5 to 0.5
- receiver_slot: int32 [1048576], P(('hi', 'lo')), may hold values from 0 to 8191, as said below
Outputs:
- displacement: bfloat16 [1048576, 128], P(('hi', 'lo'))
Inputs may be any that keep to these rules, and one draw needn't show every extreme that they name: `source_order`: each aligned block of 8192 entries is a permutation of 0 to 8191. `receiver_slot`: each aligned block of 8192 entries is a permutation of 0 to 8191.
All inputs are finite; a program needn't handle non-finite values.
Results may differ from a plain program's by a relative error of at most 0.019.
Values may be sent and summed in bfloat16 or wider, within the bound.
A program may use at most 64 MiB of HBM per device.

v0:
```python
import jax
import jax.numpy as jnp
from jax import lax
from jax.sharding import PartitionSpec as P

LEAF = 64


def partner_2(value, axis, bit):
    mask = 2**bit
    pairs = [(source, source ^ mask) for source in range(lax.axis_size(axis))]
    return lax.ppermute(value, axis, pairs)


def real_form(block_piece):
    rank_size = block_piece.shape[0]
    real_part = block_piece[:, :rank_size]
    imag_part = block_piece[:, rank_size:]
    lower_rows = jnp.concatenate([-imag_part, real_part], axis=1)
    return jnp.concatenate([block_piece, lower_rows], axis=0)


def times_factor(values, factor):
    rank_size = factor.shape[-1] // 2
    widened = factor.astype(jnp.float32)[:, None, :]
    factor_re = widened[..., :rank_size]
    factor_im = widened[..., rank_size:]
    values_re = values[..., :rank_size]
    values_im = values[..., rank_size:]
    return jnp.concatenate(
        [
            values_re * factor_re - values_im * factor_im,
            values_re * factor_im + values_im * factor_re,
        ],
        axis=-1,
    )


def apply_matrix(coeffs, matrix):
    pair_width = coeffs.shape[-1]
    flattened = coeffs.reshape(-1, pair_width)
    return jnp.dot(flattened, real_form(matrix), preferred_element_type=jnp.float32).reshape(
        coeffs.shape
    )


def mix_halves(lower_half, upper_half, matrices):
    child_zero = apply_matrix(lower_half, matrices[0, 0]) + apply_matrix(upper_half, matrices[0, 1])
    child_one = apply_matrix(lower_half, matrices[1, 0]) + apply_matrix(upper_half, matrices[1, 1])
    return (child_zero, child_one)


def local_level(coeffs, factor, matrices, stride):
    blocks_here = coeffs.shape[0]
    half_index = jnp.arange(blocks_here // 2, dtype=jnp.int32)
    lower_index = half_index // stride * (2 * stride) + half_index % stride
    upper_index = lower_index + stride
    child_zero, child_one = mix_halves(coeffs[lower_index], coeffs[upper_index], matrices)
    blocks = jnp.arange(blocks_here, dtype=jnp.int32)
    child_bit = blocks // stride % 2
    position = child_bit * (blocks_here // 2) + blocks // (2 * stride) * stride + blocks % stride
    merged = jnp.concatenate([child_zero, child_one], axis=0)[position]
    return times_factor(merged, factor).astype(jnp.bfloat16)


def remote_level(coeffs, partner, factor, matrices, own_child):
    own_row = lax.dynamic_index_in_dim(matrices, own_child, 0, keepdims=False)
    own_matrix = lax.dynamic_index_in_dim(own_row, own_child, 0, keepdims=False)
    other_matrix = lax.dynamic_index_in_dim(own_row, 1 - own_child, 0, keepdims=False)
    summed = apply_matrix(coeffs, own_matrix) + apply_matrix(partner, other_matrix)
    return times_factor(summed, factor).astype(jnp.bfloat16)


def per_device(
    charges,
    source_order,
    source_interp,
    factors,
    transfers,
    level_bits,
    receiver_interp,
    receiver_slot,
):
    points, twice_rhs = charges.shape
    rhs_count = twice_rhs // 2
    pair_width = source_interp.shape[1]
    rank_size = pair_width // 2
    blocks_here = points // LEAF
    ordered = charges[source_order].reshape(blocks_here, LEAF, twice_rhs)
    products = jnp.einsum(
        "bmk,bmr->bkr",
        ordered,
        source_interp.reshape(blocks_here, LEAF, pair_width),
        preferred_element_type=jnp.float32,
    )
    real_part = products[:, :rhs_count, :rank_size] - products[:, rhs_count:, rank_size:]
    imag_part = products[:, :rhs_count, rank_size:] + products[:, rhs_count:, :rank_size]
    coeffs = jnp.concatenate([real_part, imag_part], axis=-1).astype(jnp.bfloat16)
    strides = jnp.left_shift(jnp.int32(1), level_bits)
    coeffs = local_level(coeffs, factors[:, 0], transfers[0], strides[0])
    coeffs = local_level(coeffs, factors[:, 1], transfers[1], strides[1])
    inner_bit = lax.axis_size("lo").bit_length() - 2
    outer_bit = lax.axis_size("hi").bit_length() - 2
    inner_child = lax.axis_index("lo") >> inner_bit & 1
    outer_child = lax.axis_index("hi") >> outer_bit & 1
    partner = partner_2(coeffs, "lo", inner_bit)
    coeffs = remote_level(coeffs, partner, factors[:, 2], transfers[2], inner_child)
    partner = partner_2(coeffs, "hi", outer_bit)
    coeffs = remote_level(coeffs, partner, factors[:, 3], transfers[3], outer_child)
    carried = factors[:, 4:]
    coeffs, carried = (
        lax.all_to_all(coeffs, ("hi", "lo"), split_axis=0, concat_axis=0, tiled=True),
        lax.all_to_all(carried, ("hi", "lo"), split_axis=0, concat_axis=0, tiled=True),
    )
    coeffs = local_level(coeffs, carried[:, 0], transfers[4], strides[2])
    coeffs = local_level(coeffs, carried[:, 1], transfers[5], strides[3])
    partner = partner_2(coeffs, "lo", inner_bit)
    coeffs = remote_level(coeffs, partner, carried[:, 2], transfers[6], inner_child)
    partner = partner_2(coeffs, "hi", outer_bit)
    coeffs = remote_level(coeffs, partner, carried[:, 3], transfers[7], outer_child)
    coeff_re = coeffs[..., :rank_size]
    coeff_im = coeffs[..., rank_size:]
    stacked = jnp.concatenate(
        [
            jnp.concatenate([coeff_re, -coeff_im], axis=-1),
            jnp.concatenate([coeff_im, coeff_re], axis=-1),
        ],
        axis=1,
    )
    values = jnp.einsum(
        "bmr,bnr->bmn",
        receiver_interp.reshape(blocks_here, LEAF, pair_width),
        stacked,
        preferred_element_type=jnp.float32,
    )
    tree_values = values.astype(jnp.bfloat16).reshape(points, twice_rhs)
    return tree_values[receiver_slot]


def solution(mesh):
    return jax.shard_map(
        per_device,
        mesh=mesh,
        in_specs=(
            P(("hi", "lo"), None),
            P(("hi", "lo")),
            P(("hi", "lo"), None),
            P(("hi", "lo"), None, None),
            P(),
            P(),
            P(("hi", "lo"), None),
            P(("hi", "lo")),
        ),
        out_specs=P(("hi", "lo"), None),
        check_vma=False,
    )
```

profile of v0, /device:TPU:0, one launch (start us, length us, event | category | flops | bytes accessed | tf_op | source)
XLA Modules:
  0.0 456.0 jit_solution(6214972059677866901)
XLA Ops:
  8.8 30.1 %gather_fusion = bf16[8192,128]{1,0:T(8,128)(2,1)} fusion(bf16[8192,128]{1,0:T(8,128)(2,1)} %param.8, s32[8192]{0:T(1024)S(1)} %fusion.8), kind=kCustom, calls=%fused_computation | custom fusion | bytes 4227072 | tf_op jit(solution)/shard_map/gather | solution.py:89
  38.9 2.9 fusion.187
  41.9 2.6 fusion.1
  44.5 2.5 pad_maximum_fusion.4
  55.7 2.5 pad_maximum_fusion
  58.2 5.0 %gather_fusion.3 = f32[128,64,128]{2,1,0:T(8,128)} fusion(f32[128,64,128]{2,1,0:T(8,128)} %pad_maximum_fusion, s32[1024]{0:T(1024)S(1)} %pad_clamp_fusion.9), kind=kCustom, calls=%fused_computation.3 | custom fusion | bytes 8389120 | tf_op jit(solution)/shard_map/gather | solution.py:62
  63.5 5.0 %subtract_convert_fusion.3 = (bf16[128,64,64]{2,1,0:T(8,128)(2,1)S(1)}, bf16[128,64,64]{2,1,0:T(8,128)(2,1)S(1)}) fusion(f32[128,64,128]{2,1,0:T(8,128)} %gather_fusion.3, f32[128,64]{1,0:T(8,128)S(1)} %bitcast.218, f32[128,64]{1,0:T(8,128)S(1)} %bitcast.219), kind=kLoop, calls=%fused_computation.30 | loop fusion | flops 4194304 | bytes 6356992 | tf_op jit(solution)/shard_map/convert.14
  68.6 2.5 pad_maximum_fusion.5
  78.0 2.5 pad_maximum_fusion.1
  80.5 5.0 %gather_fusion.6 = f32[128,64,128]{2,1,0:T(8,128)} fusion(f32[128,64,128]{2,1,0:T(8,128)} %pad_maximum_fusion.1, s32[1024]{0:T(1024)S(1)} %pad_clamp_fusion.6), kind=kCustom, calls=%fused_computation.6 | custom fusion | bytes 8389120 | tf_op jit(solution)/shard_map/gather | solution.py:62
  85.5 5.0 %subtract_convert_fusion.2 = (bf16[128,64,64]{2,1,0:T(8,128)(2,1)S(1)}, bf16[128,64,64]{2,1,0:T(8,128)(2,1)S(1)}) fusion(f32[128,64,128]{2,1,0:T(8,128)} %gather_fusion.6, f32[128,64]{1,0:T(8,128)S(1)} %bitcast.215, f32[128,64]{1,0:T(8,128)S(1)} %bitcast.214), kind=kLoop, calls=%fused_computation.28 | loop fusion | flops 4194304 | bytes 6356992 | tf_op jit(solution)/shard_map/convert.12
  96.4 43.3 %collective-permute-done = bf16[128,64,128]{2,1,0:T(8,128)(2,1)} collective-permute-done((bf16[128,64,128]{2,1,0:T(8,128)(2,1)S(1)}, bf16[128,64,128]{2,1,0:T(8,128)(2,1)}, u32[]{:S(2)}, u32[]{:S(2)}) %collective-permute-start) | collective-permute-done | bytes 2097184 | tf_op jit(solution)/shard_map/ppermute | solution.py:12
  139.7 3.4 convolution_add_fusion.3
  145.3 3.7 collective-permute-start.1
  149.7 8.1 %all-to-all-start.1 = ((bf16[128,4,128]{2,1,0:T(4,128)(2,1)}), bf16[128,4,128]{2,1,0:T(4,128)(2,1)S(1)}, u32[]{:S(2)}, u32[]{:S(2)}) async-start(bf16[128,4,128]{2,1,0:T(4,128)(2,1)} %slice.446), calls=%async_computation.1 | async-start | bytes 262144 | tf_op jit(solution)/shard_map/all_to_all | solution.py:113
  167.4 28.0 %collective-permute-done.1 = bf16[128,64,128]{0,2,1:T(8,128)(2,1)} collective-permute-done((bf16[128,64,128]{0,2,1:T(8,128)(2,1)}, bf16[128,64,128]{0,2,1:T(8,128)(2,1)}, u32[]{:S(2)}, u32[]{:S(2)}) %collective-permute-start.1) | collective-permute-done | bytes 2097184 | tf_op jit(solution)/shard_map/ppermute | solution.py:12
  198.5 2.8 copy.77
  201.3 11.4 %all-to-all-start = ((bf16[128,64,128]{2,1,0:T(8,128)(2,1)}), bf16[128,64,128]{2,1,0:T(8,128)(2,1)}, u32[]{:S(2)}, u32[]{:S(2)}) async-start(bf16[128,64,128]{2,1,0:T(8,128)(2,1)} %copy.77), calls=%async_computation | async-start | bytes 4194304 | tf_op jit(solution)/shard_map/all_to_all | solution.py:112
  213.8 29.0 %all-to-all-done = bf16[128,64,128]{2,1,0:T(8,128)(2,1)} async-done(((bf16[128,64,128]{2,1,0:T(8,128)(2,1)}), bf16[128,64,128]{2,1,0:T(8,128)(2,1)}, u32[]{:S(2)}, u32[]{:S(2)}) %all-to-all-start) | async-done | bytes 2097184 | tf_op jit(solution)/shard_map/all_to_all | solution.py:112
  253.8 2.5 pad_maximum_fusion.2
  256.3 5.0 %gather_fusion.9 = f32[128,64,128]{2,1,0:T(8,128)} fusion(f32[128,64,128]{2,1,0:T(8,128)} %pad_maximum_fusion.2, s32[1024]{0:T(1024)S(1)} %pad_clamp_fusion.3), kind=kCustom, calls=%fused_computation.9 | custom fusion | bytes 8389120 | tf_op jit(solution)/shard_map/gather | solution.py:62
  261.3 5.0 %subtract_convert_fusion.1 = (bf16[128,64,64]{2,1,0:T(8,128)(2,1)S(1)}, bf16[128,64,64]{2,1,0:T(8,128)(2,1)S(1)}) fusion(f32[128,64,128]{2,1,0:T(8,128)} %gather_fusion.9, f32[128,64]{1,0:T(8,128)S(1)} %bitcast.216, f32[128,64]{1,0:T(8,128)S(1)} %bitcast.217), kind=kLoop, calls=%fused_computation.26 | loop fusion | flops 4194304 | bytes 6356992 | tf_op jit(solution)/shard_map/convert.6
  275.5 2.5 pad_maximum_fusion.3
  278.0 5.0 %gather_fusion.12 = f32[128,64,128]{2,1,0:T(8,128)} fusion(f32[128,64,128]{2,1,0:T(8,128)} %pad_maximum_fusion.3, s32[1024]{0:T(1024)S(1)} %pad_clamp_fusion), kind=kCustom, calls=%fused_computation.12 | custom fusion | bytes 8389120 | tf_op jit(solution)/shard_map/gather | solution.py:62
  283.0 5.0 %subtract_convert_fusion = (bf16[128,64,64]{2,1,0:T(8,128)(2,1)S(1)}, bf16[128,64,64]{2,1,0:T(8,128)(2,1)S(1)}) fusion(f32[128,64,128]{2,1,0:T(8,128)} %gather_fusion.12, f32[128,64]{1,0:T(8,128)S(1)} %bitcast.213, f32[128,64]{1,0:T(8,128)S(1)} %bitcast.212), kind=kLoop, calls=%fused_computation.24 | loop fusion | flops 4194304 | bytes 6356992 | tf_op jit(solution)/shard_map/convert.4
  291.9 44.9 %collective-permute-done.2 = bf16[128,64,128]{2,1,0:T(8,128)(2,1)} collective-permute-done((bf16[128,64,128]{2,1,0:T(8,128)(2,1)S(1)}, bf16[128,64,128]{2,1,0:T(8,128)(2,1)}, u32[]{:S(2)}, u32[]{:S(2)}) %collective-permute-start.2) | collective-permute-done | bytes 2097184 | tf_op jit(solution)/shard_map/ppermute | solution.py:12
  336.8 3.4 convolution_add_fusion.2
  344.2 46.3 %collective-permute-done.3 = bf16[128,64,128]{0,2,1:T(8,128)(2,1)} collective-permute-done((bf16[128,64,128]{0,2,1:T(8,128)(2,1)}, bf16[128,64,128]{0,2,1:T(8,128)(2,1)}, u32[]{:S(2)}, u32[]{:S(2)}) %collective-permute-start.3) | collective-permute-done | bytes 2097184 | tf_op jit(solution)/shard_map/ppermute | solution.py:12
  394.1 18.0 %maximum_maximum_fusion = bf16[128,128,128]{0,2,1:T(8,128)(2,1)} fusion(bf16[128,64,64]{0,2,1:T(8,128)(2,1)S(1)} %subtract_convert_fusion.4, bf16[128,64,64]{0,2,1:T(8,128)(2,1)S(1)} %get-tuple-element.6, bf16[128,64,64]{0,2,1:T(8,128)(2,1)S(1)} %get-tuple-element.5), kind=kLoop, calls=%fused_computation.22 | loop fusion | flops 16777216 | bytes 7340032 | tf_op jit(solution)/shard_map/concatenate | solution.py:123
  412.1 6.9 %copy.90 = bf16[128,128,128]{2,1,0:T(8,128)(2,1)} copy(bf16[128,128,128]{0,2,1:T(8,128)(2,1)} %maximum_maximum_fusion) | data formatting | bytes 8388608 | tf_op jit(solution)/shard_map/concatenate | solution.py:123
  419.0 6.5 %convolution_convert_fusion = bf16[128,128,64]{1,2,0:T(8,128)(2,1)} fusion(bf16[128,128,128]{2,1,0:T(8,128)(2,1)} %copy.90, bf16[128,64,128]{2,1,0:T(8,128)(2,1)S(1)} %bitcast.195), kind=kOutput, calls=%fused_computation.57 | convolution fusion | flops 269484032 | bytes 8388608 | tf_op jit(solution)/shard_map/bmr,bnr->bmn/dot_general | solution.py:130
  425.5 30.3 %gather_fusion.13 = bf16[8192,128]{1,0:T(8,128)(2,1)} fusion(bf16[8192,128]{1,0:T(8,128)(2,1)} %bitcast.193, s32[8192]{0:T(1024)S(1)} %fusion.9), kind=kCustom, calls=%fused_computation.13 | custom fusion | bytes 4227072 | tf_op jit(solution)/shard_map/gather | solution.py:137
  (133 shorter events, 68.2 us)
Async XLA Ops:
  0.0 38.9 %copy-start = (bf16[8192,128]{1,0:T(8,128)(2,1)S(1)}, bf16[8192,128]{1,0:T(8,128)(2,1)}, u32[]{:S(2)}) copy-start(bf16[8192,128]{1,0:T(8,128)(2,1)} %param.10) | copy-start | bytes 6291460
  41.9 2.6 copy-start.5
  47.0 6.3 %copy-start.4 = (bf16[128,8,128]{2,1,0:T(8,128)(2,1)S(1)}, bf16[128,8,128]{2,1,0:T(8,128)(2,1)}, u32[]{:S(2)}) copy-start(bf16[128,8,128]{2,1,0:T(8,128)(2,1)} %param.11) | copy-start | bytes 786436
  91.9 47.8 %collective-permute-start = (bf16[128,64,128]{2,1,0:T(8,128)(2,1)S(1)}, bf16[128,64,128]{2,1,0:T(8,128)(2,1)}, u32[]{:S(2)}, u32[]{:S(2)}) collective-permute-start(bf16[128,64,128]{2,1,0:T(8,128)(2,1)S(1)} %pad_maximum_fusion.6), channel_id=1, source_target_pairs={{0,8},{1,9},{2,10},{3,11},{4,12},{5,13},{6,14},{7,15},{8,0},{9,1},... | collective-permute-start | bytes 6291464 | tf_op jit(solution)/shard_map/ppermute | solution.py:12
  145.3 50.1 %collective-permute-start.1 = (bf16[128,64,128]{0,2,1:T(8,128)(2,1)}, bf16[128,64,128]{0,2,1:T(8,128)(2,1)}, u32[]{:S(2)}, u32[]{:S(2)}) collective-permute-start(bf16[128,64,128]{0,2,1:T(8,128)(2,1)} %pad_maximum_fusion.7), channel_id=1, source_target_pairs={{0,64},{16,80},{32,96},{48,112},{64,0},{80,16},{96,32},{112,48},{1... | collective-permute-start | bytes 6291464 | tf_op jit(solution)/shard_map/ppermute | solution.py:12
  149.7 51.6 %all-to-all-start.1 = ((bf16[128,4,128]{2,1,0:T(4,128)(2,1)}), bf16[128,4,128]{2,1,0:T(4,128)(2,1)S(1)}, u32[]{:S(2)}, u32[]{:S(2)}) async-start(bf16[128,4,128]{2,1,0:T(4,128)(2,1)} %slice.446), calls=%async_computation.1 | async-start | bytes 262144 | tf_op jit(solution)/shard_map/all_to_all | solution.py:113
  201.3 41.5 %all-to-all-start = ((bf16[128,64,128]{2,1,0:T(8,128)(2,1)}), bf16[128,64,128]{2,1,0:T(8,128)(2,1)}, u32[]{:S(2)}, u32[]{:S(2)}) async-start(bf16[128,64,128]{2,1,0:T(8,128)(2,1)} %copy.77), calls=%async_computation | async-start | bytes 4194304 | tf_op jit(solution)/shard_map/all_to_all | solution.py:112
  251.1 2.2 copy-start.2
  289.2 47.6 %collective-permute-start.2 = (bf16[128,64,128]{2,1,0:T(8,128)(2,1)S(1)}, bf16[128,64,128]{2,1,0:T(8,128)(2,1)}, u32[]{:S(2)}, u32[]{:S(2)}) collective-permute-start(bf16[128,64,128]{2,1,0:T(8,128)(2,1)S(1)} %pad_maximum_fusion.10), channel_id=1, source_target_pairs={{0,8},{1,9},{2,10},{3,11},{4,12},{5,13},{6,14},{7,15},{8,0},{9,1},... | collective-permute-start | bytes 6291464 | tf_op jit(solution)/shard_map/ppermute | solution.py:12
  340.8 2.4 copy-start.6
  342.4 48.2 %collective-permute-start.3 = (bf16[128,64,128]{0,2,1:T(8,128)(2,1)}, bf16[128,64,128]{0,2,1:T(8,128)(2,1)}, u32[]{:S(2)}, u32[]{:S(2)}) collective-permute-start(bf16[128,64,128]{0,2,1:T(8,128)(2,1)} %pad_maximum_fusion.11), channel_id=1, source_target_pairs={{0,64},{16,80},{32,96},{48,112},{64,0},{80,16},{96,32},{112,48},{1... | collective-permute-start | bytes 6291464 | tf_op jit(solution)/shard_map/ppermute | solution.py:12
  412.1 6.9 %copy-start.3 = (bf16[8192,128]{1,0:T(8,128)(2,1)S(1)}, bf16[8192,128]{1,0:T(8,128)(2,1)}, u32[]{:S(2)}) copy-start(bf16[8192,128]{1,0:T(8,128)(2,1)} %param.14) | copy-start | bytes 6291460
  425.5 30.3 %copy-start.1 = (bf16[8192,128]{1,0:T(8,128)(2,1)S(1)}, bf16[8192,128]{1,0:T(8,128)(2,1)}, u32[]{:S(2)}) copy-start(bf16[8192,128]{1,0:T(8,128)(2,1)} %param.10) | copy-start | bytes 6291460
where the time goes:
time: 460 us; the launch traced here: 456 us
  waiting for transfers between devices  192 us (42%)
  local copies, waits for them, and re-layouts  113 us (25%)
  other arithmetic  76 us (17%)
  matrix products  38 us (8%)
  starting transfers between devices  26.1 us (6%)
  between operations  11.2 us (2%)
    ppermute x4, waiting for transfers between devices, partner_2(): return lax.ppermute(value, axis, pairs)  163 us
    gather x1, local copies, waits for them, and re-layouts, per_device(): return tree_values[receiver_slot]  30.3 us
    gather x1, local copies, waits for them, and re-layouts, per_device(): ordered = charges[source_order].reshape(blocks_here, LEAF, twice_rhs)  30.1 us
    all_to_all x1, waiting for transfers between devices, per_device(): lax.all_to_all(coeffs, ('hi', 'lo'), split_axis=0, concat_axis=0, tiled=T...  29 us
    dot_general x24, matrix products, apply_matrix(): jnp.dot(flattened, real_form(matrix), preferred_element_type=jnp.float32)  28.5 us
    another operation x8, other arithmetic  24.4 us
    gather x4, local copies, waits for them, and re-layouts, local_level(): merged = jnp.concatenate([child_zero, child_one], axis=0)[position]  20 us
    concatenate x1, other arithmetic, per_device(): jnp.concatenate([jnp.concatenate([coeff_re, -coeff_im], axis=-1), jnp.con...  18 us
  transfers between devices with their start and end apart: 6, of which 5 were waited for; matrix products, arithmetic and copies ran while one was open for 4% of the time, Pallas kernels for 0%

commit v1 on v0

--- a/solution.py
+++ b/solution.py
@@ -63,6 +63,14 @@
     return times_factor(merged, factor).astype(jnp.bfloat16)
 
 
+def static_level(coeffs, factor, matrices, stride):
+    blocks_here, rows, width = coeffs.shape
+    grouped = coeffs.reshape(blocks_here // (2 * stride), 2, stride, rows, width)
+    child_zero, child_one = mix_halves(grouped[:, 0], grouped[:, 1], matrices)
+    merged = jnp.stack([child_zero, child_one], axis=1).reshape(coeffs.shape)
+    return times_factor(merged, factor).astype(jnp.bfloat16)
+
+
 def remote_level(coeffs, partner, factor, matrices, own_child):
     own_row = lax.dynamic_index_in_dim(matrices, own_child, 0, keepdims=False)
     own_matrix = lax.dynamic_index_in_dim(own_row, own_child, 0, keepdims=False)
@@ -103,21 +111,21 @@
     outer_bit = lax.axis_size("hi").bit_length() - 2
     inner_child = lax.axis_index("lo") >> inner_bit & 1
     outer_child = lax.axis_index("hi") >> outer_bit & 1
-    partner = partner_2(coeffs, "lo", inner_bit)
-    coeffs = remote_level(coeffs, partner, factors[:, 2], transfers[2], inner_child)
-    partner = partner_2(coeffs, "hi", outer_bit)
-    coeffs = remote_level(coeffs, partner, factors[:, 3], transfers[3], outer_child)
-    carried = factors[:, 4:]
+    carried = factors[:, 2:]
     coeffs, carried = (
         lax.all_to_all(coeffs, ("hi", "lo"), split_axis=0, concat_axis=0, tiled=True),
         lax.all_to_all(carried, ("hi", "lo"), split_axis=0, concat_axis=0, tiled=True),
     )
-    coeffs = local_level(coeffs, carried[:, 0], transfers[4], strides[2])
-    coeffs = local_level(coeffs, carried[:, 1], transfers[5], strides[3])
+    lo_stride = 2**inner_bit
+    hi_stride = lax.axis_size("lo") * 2**outer_bit
+    coeffs = static_level(coeffs, carried[:, 0], transfers[2], lo_stride)
+    coeffs = static_level(coeffs, carried[:, 1], transfers[3], hi_stride)
+    coeffs = local_level(coeffs, carried[:, 2], transfers[4], strides[2])
+    coeffs = local_level(coeffs, carried[:, 3], transfers[5], strides[3])
     partner = partner_2(coeffs, "lo", inner_bit)
-    coeffs = remote_level(coeffs, partner, carried[:, 2], transfers[6], inner_child)
+    coeffs = remote_level(coeffs, partner, carried[:, 4], transfers[6], inner_child)
     partner = partner_2(coeffs, "hi", outer_bit)
-    coeffs = remote_level(coeffs, partner, carried[:, 3], transfers[7], outer_child)
+    coeffs = remote_level(coeffs, partner, carried[:, 5], transfers[7], outer_child)
     coeff_re = coeffs[..., :rank_size]
     coeff_im = coeffs[..., rank_size:]
     stacked = jnp.concatenate(

time: 460 us -> 387 us (0.84)
  waiting for transfers between devices: 192 us -> 117 us
  other arithmetic: 76 us -> 89 us
  matrix products: 38 us -> 30.5 us
    ppermute x4 -> x2, waiting for transfers between devices: 163 us -> 91.2 us  [partner_2(): return lax.ppermute(value, axis, pairs)]
    dot_general x24 -> x28, matrix products: 28.5 us -> 21 us  [apply_matrix(): jnp.dot(flattened, real_form(matrix), preferred_element_type=jnp.float32)]
    ppermute x4 -> x2, starting transfers between devices: 6.65 us -> 0.75 us  [partner_2(): return lax.ppermute(value, axis, pairs)]
    another operation x8 -> x10, other arithmetic: 24.4 us -> 27.3 us
    concatenate x7 -> x6, other arithmetic: 10.6 us -> 13 us  [times_factor(): jnp.concatenate([values_re * factor_re - values_im * factor_im, values_re...]
  transfers between devices with their start and end apart: 6 -> 4, of which waited for: 5 -> 3; matrix products, arithmetic and copies ran while one was open for 4% -> 27% of each run, Pallas kernels for 0% -> 0%
where the time goes in v1:
time: 387 us; the launch traced here: 382 us
  waiting for transfers between devices  117 us (30%)
  local copies, waits for them, and re-layouts  112 us (29%)
  other arithmetic  89 us (23%)
  matrix products  30.5 us (8%)
  starting transfers between devices  21.7 us (6%)
  between operations  10.7 us (3%)
    ppermute x2, waiting for transfers between devices, partner_2(): return lax.ppermute(value, axis, pairs)  91.2 us
    gather x1, local copies, waits for them, and re-layouts, per_device(): return tree_values[receiver_slot]  30.3 us
    gather x1, local copies, waits for them, and re-layouts, per_device(): ordered = charges[source_order].reshape(blocks_here, LEAF, twice_rhs)  30.1 us
    another operation x8, other arithmetic  26.3 us
    all_to_all x1, waiting for transfers between devices, per_device(): lax.all_to_all(coeffs, ('hi', 'lo'), split_axis=0, concat_axis=0, tiled=T...  26.2 us
    dot_general x28, matrix products, apply_matrix(): jnp.dot(flattened, real_form(matrix), preferred_element_type=jnp.float32)  21 us
    gather x4, local copies, waits for them, and re-layouts, local_level(): merged = jnp.concatenate([child_zero, child_one], axis=0)[position]  20.2 us
    concatenate x1, other arithmetic, per_device(): jnp.concatenate([jnp.concatenate([coeff_re, -coeff_im], axis=-1), jnp.con...  18 us
  transfers between devices with their start and end apart: 4, of which 3 were waited for; matrix products, arithmetic and copies ran while one was open for 27% of the time, Pallas kernels for 0%

profile of v1, /device:TPU:0, one launch (start us, length us, event | category | flops | bytes accessed | tf_op | source)
XLA Modules:
  0.0 381.6 jit_solution(5247367796997308078)
XLA Ops:
  1.9 11.1 %all-to-all-start.1 = ((bf16[128,6,128]{2,1,0:T(8,128)(2,1)}), bf16[128,6,128]{2,1,0:T(8,128)(2,1)S(1)}, u32[]{:S(2)}, u32[]{:S(2)}) async-start(bf16[128,6,128]{2,1,0:T(8,128)(2,1)} %slice.487), calls=%async_computation.1 | async-start | bytes 524288 | tf_op jit(solution)/shard_map/all_to_all | solution.py:117
  26.2 30.1 %gather_fusion = bf16[8192,128]{1,0:T(8,128)(2,1)} fusion(bf16[8192,128]{1,0:T(8,128)(2,1)} %param.8, s32[8192]{0:T(1024)S(1)} %fusion.10), kind=kCustom, calls=%fused_computation | custom fusion | bytes 4227072 | tf_op jit(solution)/shard_map/gather | solution.py:97
  56.3 2.9 fusion.212
  59.3 2.6 fusion.1
  61.9 2.5 pad_maximum_fusion.6
  72.8 2.5 pad_maximum_fusion
  75.3 5.0 %gather_fusion.3 = f32[128,64,128]{2,1,0:T(8,128)} fusion(f32[128,64,128]{2,1,0:T(8,128)} %pad_maximum_fusion, s32[1024]{0:T(1024)S(1)} %pad_clamp_fusion.9), kind=kCustom, calls=%fused_computation.3 | custom fusion | bytes 8389120 | tf_op jit(solution)/shard_map/gather | solution.py:62
  80.7 5.0 %subtract_convert_fusion.5 = (bf16[128,64,64]{2,1,0:T(8,128)(2,1)S(1)}, bf16[128,64,64]{2,1,0:T(8,128)(2,1)S(1)}) fusion(f32[128,64,128]{2,1,0:T(8,128)} %gather_fusion.3, f32[128,64]{1,0:T(8,128)S(1)} %bitcast.294, f32[128,64]{1,0:T(8,128)S(1)} %bitcast.295), kind=kLoop, calls=%fused_computation.36 | loop fusion | flops 4194304 | bytes 6356992 | tf_op jit(solution)/shard_map/convert.16
  85.7 2.5 pad_maximum_fusion.7
  102.5 2.5 pad_maximum_fusion.1
  105.0 5.0 %gather_fusion.6 = f32[128,64,128]{2,1,0:T(8,128)} fusion(f32[128,64,128]{2,1,0:T(8,128)} %pad_maximum_fusion.1, s32[1024]{0:T(1024)S(1)} %pad_clamp_fusion.6), kind=kCustom, calls=%fused_computation.6 | custom fusion | bytes 8389120 | tf_op jit(solution)/shard_map/gather | solution.py:62
  110.0 5.0 %subtract_convert_fusion.4 = (bf16[128,64,64]{2,1,0:T(8,128)(2,1)S(1)}, bf16[128,64,64]{2,1,0:T(8,128)(2,1)S(1)}) fusion(f32[128,64,128]{2,1,0:T(8,128)} %gather_fusion.6, f32[128,64]{1,0:T(8,128)S(1)} %bitcast.287, f32[128,64]{1,0:T(8,128)S(1)} %bitcast.286), kind=kLoop, calls=%fused_computation.34 | loop fusion | flops 4194304 | bytes 6356992 | tf_op jit(solution)/shard_map/convert.14
  115.6 2.9 pad_maximum_fusion.8
  118.5 9.8 %all-to-all-start = ((bf16[128,64,128]{2,1,0:T(8,128)(2,1)}), bf16[128,64,128]{2,1,0:T(8,128)(2,1)S(1)}, u32[]{:S(2)}, u32[]{:S(2)}) async-start(bf16[128,64,128]{2,1,0:T(8,128)(2,1)} %pad_maximum_fusion.8), calls=%async_computation | async-start | bytes 4194304 | tf_op jit(solution)/shard_map/all_to_all | solution.py:116
  132.6 26.2 %all-to-all-done = bf16[128,64,128]{2,1,0:T(8,128)(2,1)S(1)} async-done(((bf16[128,64,128]{2,1,0:T(8,128)(2,1)}), bf16[128,64,128]{2,1,0:T(8,128)(2,1)S(1)}, u32[]{:S(2)}, u32[]{:S(2)}) %all-to-all-start) | async-done | bytes 2097184 | tf_op jit(solution)/shard_map/all_to_all | solution.py:116
  169.1 2.5 pad_maximum_fusion.9
  174.1 2.5 gather_fusion.8
  178.5 2.7 pad_maximum_fusion.4
  181.2 5.1 %gather_fusion.9 = f32[128,64,128]{2,1,0:T(8,128)} fusion(f32[128,64,128]{2,1,0:T(8,128)} %pad_maximum_fusion.4, s32[1024]{0:T(1024)} %pad_clamp_fusion.3), kind=kCustom, calls=%fused_computation.9 | custom fusion | bytes 8389120 | tf_op jit(solution)/shard_map/gather | solution.py:62
  186.3 5.0 %subtract_convert_fusion.1 = (bf16[128,64,64]{2,1,0:T(8,128)(2,1)S(1)}, bf16[128,64,64]{2,1,0:T(8,128)(2,1)S(1)}) fusion(f32[128,64,128]{2,1,0:T(8,128)} %gather_fusion.9, f32[128,64]{1,0:T(8,128)S(1)} %bitcast.288, f32[128,64]{1,0:T(8,128)S(1)} %bitcast.289), kind=kLoop, calls=%fused_computation.28 | loop fusion | flops 4194304 | bytes 6356992 | tf_op jit(solution)/shard_map/convert.6
  191.3 2.5 pad_maximum_fusion.10
  196.2 2.5 gather_fusion.11
  201.1 2.5 pad_maximum_fusion.5
  203.6 5.1 %gather_fusion.12 = f32[128,64,128]{2,1,0:T(8,128)} fusion(f32[128,64,128]{2,1,0:T(8,128)} %pad_maximum_fusion.5, s32[1024]{0:T(1024)} %pad_clamp_fusion), kind=kCustom, calls=%fused_computation.12 | custom fusion | bytes 8389120 | tf_op jit(solution)/shard_map/gather | solution.py:62
  208.8 5.0 %subtract_convert_fusion = (bf16[128,64,64]{2,1,0:T(8,128)(2,1)S(1)}, bf16[128,64,64]{2,1,0:T(8,128)(2,1)S(1)}) fusion(f32[128,64,128]{2,1,0:T(8,128)} %gather_fusion.12, f32[128,64]{1,0:T(8,128)S(1)} %bitcast.285, f32[128,64]{1,0:T(8,128)S(1)} %bitcast.284), kind=kLoop, calls=%fused_computation.26 | loop fusion | flops 4194304 | bytes 6356992 | tf_op jit(solution)/shard_map/convert.4
  217.5 44.9 %collective-permute-done = bf16[128,64,128]{2,1,0:T(8,128)(2,1)} collective-permute-done((bf16[128,64,128]{2,1,0:T(8,128)(2,1)S(1)}, bf16[128,64,128]{2,1,0:T(8,128)(2,1)}, u32[]{:S(2)}, u32[]{:S(2)}) %collective-permute-start) | collective-permute-done | bytes 2097184 | tf_op jit(solution)/shard_map/ppermute | solution.py:12
  262.4 3.4 convolution_add_fusion.1
  269.8 46.3 %collective-permute-done.1 = bf16[128,64,128]{0,2,1:T(8,128)(2,1)} collective-permute-done((bf16[128,64,128]{0,2,1:T(8,128)(2,1)}, bf16[128,64,128]{0,2,1:T(8,128)(2,1)}, u32[]{:S(2)}, u32[]{:S(2)}) %collective-permute-start.1) | collective-permute-done | bytes 2097184 | tf_op jit(solution)/shard_map/ppermute | solution.py:12
  319.7 18.0 %maximum_maximum_fusion = bf16[128,128,128]{0,2,1:T(8,128)(2,1)} fusion(bf16[128,64,64]{0,2,1:T(8,128)(2,1)S(1)} %subtract_convert_fusion.6, bf16[128,64,64]{0,2,1:T(8,128)(2,1)S(1)} %get-tuple-element.6, bf16[128,64,64]{0,2,1:T(8,128)(2,1)S(1)} %get-tuple-element.5), kind=kLoop, calls=%fused_computation.24 | loop fusion | flops 16777216 | bytes 7340032 | tf_op jit(solution)/shard_map/concatenate | solution.py:131
  337.6 6.9 %copy.39 = bf16[128,128,128]{2,1,0:T(8,128)(2,1)} copy(bf16[128,128,128]{0,2,1:T(8,128)(2,1)} %maximum_maximum_fusion) | data formatting | bytes 8388608 | tf_op jit(solution)/shard_map/concatenate | solution.py:131
  344.6 6.5 %convolution_convert_fusion = bf16[128,128,64]{1,2,0:T(8,128)(2,1)} fusion(bf16[128,128,128]{2,1,0:T(8,128)(2,1)} %copy.39, bf16[128,64,128]{2,1,0:T(8,128)(2,1)S(1)} %bitcast.275), kind=kOutput, calls=%fused_computation.59 | convolution fusion | flops 269484032 | bytes 8388608 | tf_op jit(solution)/shard_map/bmr,bnr->bmn/dot_general | solution.py:138
  351.1 30.3 %gather_fusion.13 = bf16[8192,128]{1,0:T(8,128)(2,1)} fusion(bf16[8192,128]{1,0:T(8,128)(2,1)} %bitcast.261, s32[8192]{0:T(1024)S(1)} %fusion.11), kind=kCustom, calls=%fused_computation.13 | custom fusion | bytes 4227072 | tf_op jit(solution)/shard_map/gather | solution.py:145
  (136 shorter events, 63.8 us)
Async XLA Ops:
  0.0 56.3 %copy-start = (bf16[8192,128]{1,0:T(8,128)(2,1)S(1)}, bf16[8192,128]{1,0:T(8,128)(2,1)}, u32[]{:S(2)}) copy-start(bf16[8192,128]{1,0:T(8,128)(2,1)} %param.10) | copy-start | bytes 6291460
  1.9 116.6 %all-to-all-start.1 = ((bf16[128,6,128]{2,1,0:T(8,128)(2,1)}), bf16[128,6,128]{2,1,0:T(8,128)(2,1)S(1)}, u32[]{:S(2)}, u32[]{:S(2)}) async-start(bf16[128,6,128]{2,1,0:T(8,128)(2,1)} %slice.487), calls=%async_computation.1 | async-start | bytes 524288 | tf_op jit(solution)/shard_map/all_to_all | solution.py:117
  59.2 2.6 copy-start.3
  118.5 40.2 %all-to-all-start = ((bf16[128,64,128]{2,1,0:T(8,128)(2,1)}), bf16[128,64,128]{2,1,0:T(8,128)(2,1)S(1)}, u32[]{:S(2)}, u32[]{:S(2)}) async-start(bf16[128,64,128]{2,1,0:T(8,128)(2,1)} %pad_maximum_fusion.8), calls=%async_computation | async-start | bytes 4194304 | tf_op jit(solution)/shard_map/all_to_all | solution.py:116
  158.7 1.2 copy-start.7
  158.7 1.3 copy-start.8
  198.7 0.7 copy-start.5
  198.7 0.7 copy-start.6
  199.9 0.7 copy-start.4
  215.0 47.4 %collective-permute-start = (bf16[128,64,128]{2,1,0:T(8,128)(2,1)S(1)}, bf16[128,64,128]{2,1,0:T(8,128)(2,1)}, u32[]{:S(2)}, u32[]{:S(2)}) collective-permute-start(bf16[128,64,128]{2,1,0:T(8,128)(2,1)S(1)} %pad_maximum_fusion.11), channel_id=1, source_target_pairs={{0,8},{1,9},{2,10},{3,11},{4,12},{5,13},{6,14},{7,15},{8,0},{9,1},... | collective-permute-start | bytes 6291464 | tf_op jit(solution)/shard_map/ppermute | solution.py:12
  266.4 2.5 copy-start.9
  267.9 48.2 %collective-permute-start.1 = (bf16[128,64,128]{0,2,1:T(8,128)(2,1)}, bf16[128,64,128]{0,2,1:T(8,128)(2,1)}, u32[]{:S(2)}, u32[]{:S(2)}) collective-permute-start(bf16[128,64,128]{0,2,1:T(8,128)(2,1)} %pad_maximum_fusion.12), channel_id=1, source_target_pairs={{0,64},{16,80},{32,96},{48,112},{64,0},{80,16},{96,32},{112,48},{1... | collective-permute-start | bytes 6291464 | tf_op jit(solution)/shard_map/ppermute | solution.py:12
  337.6 6.9 %copy-start.2 = (bf16[8192,128]{1,0:T(8,128)(2,1)S(1)}, bf16[8192,128]{1,0:T(8,128)(2,1)}, u32[]{:S(2)}) copy-start(bf16[8192,128]{1,0:T(8,128)(2,1)} %param.14) | copy-start | bytes 6291460
  351.1 30.3 %copy-start.1 = (bf16[8192,128]{1,0:T(8,128)(2,1)S(1)}, bf16[8192,128]{1,0:T(8,128)(2,1)}, u32[]{:S(2)}) copy-start(bf16[8192,128]{1,0:T(8,128)(2,1)} %param.10) | copy-start | bytes 6291460

commit v2 on v1

--- a/solution.py
+++ b/solution.py
@@ -1,9 +1,82 @@
 import jax
 import jax.numpy as jnp
 from jax import lax
+from jax.experimental import pallas as pl
+from jax.experimental.pallas import tpu as pltpu
 from jax.sharding import PartitionSpec as P
 
 LEAF = 64
+PAIRS_PER_DOT = 8
+
+
+def pair_weights(matrices):
+    def rf(m):
+        r, i = m[:, :64], m[:, 64:]
+        return jnp.concatenate([m, jnp.concatenate([-i, r], axis=1)], axis=0)
+    top = jnp.concatenate([rf(matrices[0, 0]), rf(matrices[1, 0])], axis=1)
+    bottom = jnp.concatenate([rf(matrices[0, 1]), rf(matrices[1, 1])], axis=1)
+    return jnp.concatenate([top, bottom], axis=0)
+
+
+def factor_pair(factor):
+    wide = factor.astype(jnp.float32)
+    re, im = wide[:, :64], wide[:, 64:]
+    return (jnp.concatenate([re, re], axis=1)[:, None, :],
+            jnp.concatenate([-im, im], axis=1)[:, None, :])
+
+
+def levels_kernel(bits_ref, x_ref, w_ref, a_ref, b_ref, o_ref, buf, lhs):
+    count = w_ref.shape[0]
+    blocks, rows, width = x_ref.shape
+    chunks = blocks // 2 // PAIRS_PER_DOT
+    for level in range(count):
+        src = x_ref if level == 0 else buf.at[(level - 1) % 2]
+        dst = o_ref if level == count - 1 else buf.at[level % 2]
+        bit = bits_ref[level]
+        stride = jnp.left_shift(jnp.int32(1), bit)
+
+        def pair_of(p):
+            low = jnp.left_shift(jnp.right_shift(p, bit), bit + 1) + jnp.bitwise_and(p, stride - 1)
+            return low, low + stride
+
+        def chunk(g, carry):
+            for j in range(PAIRS_PER_DOT):
+                n0, n1 = pair_of(g * PAIRS_PER_DOT + j)
+                lhs[j * rows:(j + 1) * rows, 0:width] = src[n0]
+                lhs[j * rows:(j + 1) * rows, width:2 * width] = src[n1]
+            y = jnp.dot(lhs[...], w_ref[level], preferred_element_type=jnp.float32)
+            for j in range(PAIRS_PER_DOT):
+                n0, n1 = pair_of(g * PAIRS_PER_DOT + j)
+                for half, n in ((0, n0), (1, n1)):
+                    part = y[j * rows:(j + 1) * rows, half * width:(half + 1) * width]
+                    turned = pltpu.roll(part, width // 2, 1)
+                    dst[n] = (part * a_ref[level, n] + turned * b_ref[level, n]).astype(dst.dtype)
+            return carry
+
+        lax.fori_loop(0, chunks, chunk, 0)
+
+
+def run_levels(coeffs, bits, matrices_list, factor_list):
+    count = len(matrices_list)
+    weights = jnp.stack([pair_weights(m) for m in matrices_list])
+    pairs = [factor_pair(f) for f in factor_list]
+    a = jnp.stack([p[0] for p in pairs])
+    b = jnp.stack([p[1] for p in pairs])
+    blocks, rows, width = coeffs.shape
+    vmem = pl.BlockSpec(memory_space=pltpu.VMEM)
+    return pl.pallas_call(
+        levels_kernel,
+        out_shape=jax.ShapeDtypeStruct(coeffs.shape, jnp.bfloat16),
+        in_specs=[pl.BlockSpec(memory_space=pltpu.SMEM)] + [vmem] * 4,
+        out_specs=vmem,
+        scratch_shapes=[
+            pltpu.VMEM((2, blocks, rows, width), jnp.bfloat16),
+            pltpu.VMEM((PAIRS_PER_DOT * rows, 2 * width), jnp.bfloat16),
+        ],
+        cost_estimate=pl.CostEstimate(
+            flops=count * blocks * rows * 2 * width * 2 * width,
+            bytes_accessed=2 * coeffs.size * 2, transcendentals=0),
+    )(bits, coeffs, weights, a, b)
 
 
 def partner_2(value, axis, bit):
@@ -48,27 +121,6 @@
     child_zero = apply_matrix(lower_half, matrices[0, 0]) + apply_matrix(upper_half, matrices[0, 1])
     child_one = apply_matrix(lower_half, matrices[1, 0]) + apply_matrix(upper_half, matrices[1, 1])
     return (child_zero, child_one)
-
-
-def local_level(coeffs, factor, matrices, stride):
-    blocks_here = coeffs.shape[0]
-    half_index = jnp.arange(blocks_here // 2, dtype=jnp.int32)
-    lower_index = half_index // stride * (2 * stride) + half_index % stride
-    upper_index = lower_index + stride
-    child_zero, child_one = mix_halves(coeffs[lower_index], coeffs[upper_index], matrices)
-    blocks = jnp.arange(blocks_here, dtype=jnp.int32)
-    child_bit = blocks // stride % 2
-    position = child_bit * (blocks_here // 2) + blocks // (2 * stride) * stride + blocks % stride
-    merged = jnp.concatenate([child_zero, child_one], axis=0)[position]
-    return times_factor(merged, factor).astype(jnp.bfloat16)
-
-
-def static_level(coeffs, factor, matrices, stride):
-    blocks_here, rows, width = coeffs.shape
-    grouped = coeffs.reshape(blocks_here // (2 * stride), 2, stride, rows, width)
-    child_zero, child_one = mix_halves(grouped[:, 0], grouped[:, 1], matrices)
-    merged = jnp.stack([child_zero, child_one], axis=1).reshape(coeffs.shape)
-    return times_factor(merged, factor).astype(jnp.bfloat16)
 
 
 def remote_level(coeffs, partner, factor, matrices, own_child):
@@ -104,9 +156,9 @@
     real_part = products[:, :rhs_count, :rank_size] - products[:, rhs_count:, rank_size:]
     imag_part = products[:, :rhs_count, rank_size:] + products[:, rhs_count:, :rank_size]
     coeffs = jnp.concatenate([real_part, imag_part], axis=-1).astype(jnp.bfloat16)
-    strides = jnp.left_shift(jnp.int32(1), level_bits)
-    coeffs = local_level(coeffs, factors[:, 0], transfers[0], strides[0])
-    coeffs = local_level(coeffs, factors[:, 1], transfers[1], strides[1])
+    coeffs = run_levels(
+        coeffs, level_bits[:2], [transfers[0], transfers[1]], [factors[:, 0], factors[:, 1]]
+    )
     inner_bit = lax.axis_size("lo").bit_length() - 2
     outer_bit = lax.axis_size("hi").bit_length() - 2
     inner_child = lax.axis_index("lo") >> inner_bit & 1
@@ -116,12 +168,16 @@
         lax.all_to_all(coeffs, ("hi", "lo"), split_axis=0, concat_axis=0, tiled=True),
         lax.all_to_all(carried, ("hi", "lo"), split_axis=0, concat_axis=0, tiled=True),
     )
-    lo_stride = 2**inner_bit
-    hi_stride = lax.axis_size("lo") * 2**outer_bit
-    coeffs = static_level(coeffs, carried[:, 0], transfers[2], lo_stride)
-    coeffs = static_level(coeffs, carried[:, 1], transfers[3], hi_stride)
-    coeffs = local_level(coeffs, carried[:, 2], transfers[4], strides[2])
-    coeffs = local_level(coeffs, carried[:, 3], transfers[5], strides[3])
+    hi_bit = (lax.axis_size("lo") * 2**outer_bit).bit_length() - 1
+    switched_bits = jnp.concatenate(
+        [jnp.array([inner_bit, hi_bit], jnp.int32), level_bits[2:4]]
+    )
+    coeffs = run_levels(
+        coeffs,
+        switched_bits,
+        [transfers[2], transfers[3], transfers[4], transfers[5]],
+        [carried[:, 0], carried[:, 1], carried[:, 2], carried[:, 3]],
+    )
     partner = partner_2(coeffs, "lo", inner_bit)
     coeffs = remote_level(coeffs, partner, carried[:, 4], transfers[6], inner_child)
     partner = partner_2(coeffs, "hi", outer_bit)

time: 387 us -> 292 us (0.75); the launches traced: 382 us -> 292 us
  other arithmetic: 89 us -> 35.8 us
  local copies, waits for them, and re-layouts: 112 us -> 74.4 us
  Pallas kernels: 0 us -> 24.8 us
  matrix products: 30.5 us -> 17.7 us
  between operations: 10.7 us -> 0.44 us
    gather x12 -> x0, local copies, waits for them, and re-layouts: 39.5 us -> none  [the longest x4 20.2 us: local_level(): merged = jnp.concatenate([child_zero, child_one], axis=0)[position]]
    pallas_call x0 -> x2, Pallas kernels: none -> 24.8 us  [run_levels(): pl.pallas_call(levels_kernel, out_shape=jax.ShapeDtypeStruct(coeffs.shape...]
    another operation x10 -> x20, other arithmetic: 27.3 us -> 8.85 us
    dot_general x28 -> x4, matrix products: 21 us -> 8.22 us  [apply_matrix(): jnp.dot(flattened, real_form(matrix), preferred_element_type=jnp.float32)]
    concatenate x6 -> x1, other arithmetic: 13 us -> 1.51 us  [times_factor(): jnp.concatenate([values_re * factor_re - values_im * factor_im, values_re...]
    concatenate x4 -> x7, other arithmetic: 10.2 us -> 1.08 us  [the longest x1 0.59 us: per_device(): jnp.concatenate([jnp.array([inner_bit, hi_bit], jnp.int32), level_bits[2:...]
    select_n x8 -> x0, other arithmetic: 5.93 us -> none  [the longest x2 2.98 us: local_level(): merged = jnp.concatenate([child_zero, child_one], axis=0)[position]]
    neg x24 -> x4, other arithmetic: 3.96 us -> 0.03 us  [real_form(): lower_rows = jnp.concatenate([-imag_part, real_part], axis=1)]
  transfers between devices with their start and end apart: 4 -> 4, of which waited for: 3 -> 3; matrix products, arithmetic and copies ran while one was open for 27% -> 19% of each run, Pallas kernels for 0% -> 3%
where the time goes in v2:
time: 292 us
  waiting for transfers between devices  117 us (40%)
  local copies, waits for them, and re-layouts  74.4 us (25%)
  other arithmetic  35.8 us (12%)
  Pallas kernels  24.8 us (8%)
  starting transfers between devices  21.6 us (7%)
  matrix products  17.7 us (6%)
    ppermute x2, waiting for transfers between devices, partner_2(): return lax.ppermute(value, axis, pairs)  89.7 us
    gather x1, local copies, waits for them, and re-layouts, per_device(): return tree_values[receiver_slot]  30.3 us
    gather x1, local copies, waits for them, and re-layouts, per_device(): ordered = charges[source_order].reshape(blocks_here, LEAF, twice_rhs)  30.1 us
    all_to_all x1, waiting for transfers between devices, per_device(): lax.all_to_all(coeffs, ('hi', 'lo'), split_axis=0, concat_axis=0, tiled=T...  27.4 us
    pallas_call x2, Pallas kernels, run_levels(): pl.pallas_call(levels_kernel, out_shape=jax.ShapeDtypeStruct(coeffs.shape...  24.8 us
    concatenate x1, other arithmetic, per_device(): jnp.concatenate([jnp.concatenate([coeff_re, -coeff_im], axis=-1), jnp.con...  18 us
    all_to_all x1, starting transfers between devices, per_device(): lax.all_to_all(carried, ('hi', 'lo'), split_axis=0, concat_axis=0, tiled=...  11.1 us
    all_to_all x1, starting transfers between devices, per_device(): lax.all_to_all(coeffs, ('hi', 'lo'), split_axis=0, concat_axis=0, tiled=T...  9.76 us
  transfers between devices with their start and end apart: 4, of which 3 were waited for; matrix products, arithmetic and copies ran while one was open for 19% of the time, Pallas kernels for 3%

profile of v2, /device:TPU:0, one launch (start us, length us, event | category | flops | bytes accessed | tf_op | source)
XLA Modules:
  0.0 291.8 jit_solution(17754079125810194341)
XLA Ops:
  0.0 1.9 slice.465
  1.9 11.1 %all-to-all-start.1 = ((bf16[128,6,128]{2,1,0:T(8,128)(2,1)}), bf16[128,6,128]{2,1,0:T(8,128)(2,1)S(1)}, u32[]{:S(2)}, u32[]{:S(2)}) async-start(bf16[128,6,128]{2,1,0:T(8,128)(2,1)} %slice.465), calls=%async_computation.1 | async-start | bytes 524288 | tf_op jit(solution)/shard_map/all_to_all | solution.py:169
  13.0 1.1 fusion.36
  14.2 1.1 fusion.35
  15.9 30.1 %gather_fusion = bf16[8192,128]{1,0:T(8,128)(2,1)} fusion(bf16[8192,128]{1,0:T(8,128)(2,1)} %param.9, s32[8192]{0:T(1024)S(1)} %fusion.5), kind=kCustom, calls=%fused_computation | custom fusion | bytes 4227072 | tf_op jit(solution)/shard_map/gather | solution.py:149
  46.0 2.9 %fusion.40 = f32[128,128,128]{2,1,0:T(8,128)S(1)} fusion(bf16[128,64,128]{2,1,0:T(8,128)(2,1)} %bitcast.163, bf16[128,64,128]{2,1,0:T(8,128)(2,1)S(1)} %bitcast.161), kind=kOutput, calls=%fused_computation.161 | convolution fusion | flops 268435456 | bytes 12582912 | tf_op jit(solution)/shard_map/bmk,bmr->bkr/dot_general | solution.py:150
  48.9 2.4 fusion.1
  54.3 2.5 pad_maximum_fusion.x_ref
  57.0 0.7 pad_maximum_fusion.3.w_ref
  57.7 0.7 pad_maximum_fusion.6
  58.6 0.8 pad_maximum_fusion.7.b_ref
  59.8 9.2 %shard_map.91 = bf16[128,64,128]{2,1,0:T(8,128)(2,1)} custom-call(s32[2]{0:T(128)} %get-tuple-element.133.bits_ref, bf16[128,64,128]{2,1,0:T(8,128)(2,1)} %pad_maximum_fusion.x_ref, bf16[2,256,256]{2,1,0:T(8,128)(2,1)} %pad_maximum_fusion.3.w_ref, f32[2,128,1,128]{3,2,1,0:T(1,128)} %bitcast.165, f32[2,128,1,128]{3,2,1,0:T(1,128)} %pad_maximum_fusion.7.b_ref), custom_call_target="tpu_custom_call" | custom-call | flops 1073741824 | bytes 4194304 | tf_op jit(solution)/shard_map/pallas_call | solution.py:67
  69.0 0.9 pad_maximum_fusion.2.w_ref
  69.9 9.8 %all-to-all-start = ((bf16[128,64,128]{2,1,0:T(8,128)(2,1)}), bf16[128,64,128]{2,1,0:T(8,128)(2,1)S(1)}, u32[]{:S(2)}, u32[]{:S(2)}) async-start(bf16[128,64,128]{2,1,0:T(8,128)(2,1)} %shard_map.91), calls=%async_computation | async-start | bytes 4194304 | tf_op jit(solution)/shard_map/all_to_all | solution.py:168
  81.1 0.7 pad_maximum_fusion.4
  81.8 1.0 pad_maximum_fusion.5.b_ref
  82.8 27.4 %all-to-all-done.x_ref = bf16[128,64,128]{2,1,0:T(8,128)(2,1)S(1)} async-done(((bf16[128,64,128]{2,1,0:T(8,128)(2,1)}), bf16[128,64,128]{2,1,0:T(8,128)(2,1)S(1)}, u32[]{:S(2)}, u32[]{:S(2)}) %all-to-all-start) | async-done | bytes 2097184 | tf_op jit(solution)/shard_map/all_to_all | solution.py:168
  110.1 1.3 copy-done.2
  111.5 15.6 %shard_map.92 = bf16[128,64,128]{2,1,0:T(8,128)(2,1)} custom-call(s32[4]{0:T(128)} %pad_add_fusion.bits_ref, bf16[128,64,128]{2,1,0:T(8,128)(2,1)} %copy-done.2, bf16[4,256,256]{2,1,0:T(8,128)(2,1)} %pad_maximum_fusion.2.w_ref, f32[4,128,1,128]{3,2,1,0:T(1,128)} %bitcast.174, f32[4,128,1,128]{3,2,1,0:T(1,128)} %pad_maximum_fusion.5.b_ref), custom_call_target="tpu_custom_call" | custom-call | flops 2147483648 | bytes 4194304 | tf_op jit(solution)/shard_map/pallas_call | solution.py:67
  127.8 3.3 %fusion.3 = f32[128,64,128]{0,2,1:T(8,128)S(1)} fusion(bf16[128,64,128]{2,1,0:T(8,128)(2,1)} %shard_map.92, bf16[64,64]{0,1:T(8,128)(2,1)S(1)} %get-tuple-element.82, bf16[64,64]{0,1:T(8,128)(2,1)S(1)} %get-tuple-element.81, bf16[64,128]{0,1:T(8,128)(2,1)S(1)} %bitcast.171), kind=kOutput, calls=%fused_computation.12 | convolution fusion | flops 268533760 | bytes 6324224 | tf_op jit(solution)/shard_map/dot_general | solution.py:115
  131.0 43.4 %collective-permute-done = bf16[128,64,128]{2,1,0:T(8,128)(2,1)S(1)} collective-permute-done((bf16[128,64,128]{2,1,0:T(8,128)(2,1)}, bf16[128,64,128]{2,1,0:T(8,128)(2,1)S(1)}, u32[]{:S(2)}, u32[]{:S(2)}) %collective-permute-start) | collective-permute-done | bytes 2097184 | tf_op jit(solution)/shard_map/ppermute | solution.py:85
  174.4 1.8 convolution_add_fusion.1
  176.9 1.5 pad_maximum_fusion.1
  178.4 0.7 collective-permute-start.1
  179.5 0.8 fusion.7
  180.3 46.3 %collective-permute-done.1 = bf16[128,64,128]{0,2,1:T(8,128)(2,1)} collective-permute-done((bf16[128,64,128]{0,2,1:T(8,128)(2,1)}, bf16[128,64,128]{0,2,1:T(8,128)(2,1)}, u32[]{:S(2)}, u32[]{:S(2)}) %collective-permute-start.1) | collective-permute-done | bytes 2097184 | tf_op jit(solution)/shard_map/ppermute | solution.py:85
  226.6 2.3 convolution_add_fusion
  229.4 0.6 fusion.34
  230.1 18.0 %maximum_maximum_fusion = bf16[128,128,128]{0,2,1:T(8,128)(2,1)} fusion(bf16[128,64,64]{0,2,1:T(8,128)(2,1)S(1)} %subtract_convert_fusion, bf16[128,64,64]{0,2,1:T(8,128)(2,1)S(1)} %get-tuple-element.6, bf16[128,64,64]{0,2,1:T(8,128)(2,1)S(1)} %get-tuple-element.5), kind=kLoop, calls=%fused_computation.6 | loop fusion | flops 16777216 | bytes 7340032 | tf_op jit(solution)/shard_map/concatenate | solution.py:187
  248.1 6.9 %copy.56 = bf16[128,128,128]{2,1,0:T(8,128)(2,1)} copy(bf16[128,128,128]{0,2,1:T(8,128)(2,1)} %maximum_maximum_fusion) | data formatting | bytes 8388608 | tf_op jit(solution)/shard_map/concatenate | solution.py:187
  255.0 6.5 %convolution_convert_fusion = bf16[128,128,64]{1,2,0:T(8,128)(2,1)} fusion(bf16[128,128,128]{2,1,0:T(8,128)(2,1)} %copy.56, bf16[128,64,128]{2,1,0:T(8,128)(2,1)S(1)} %bitcast.164), kind=kOutput, calls=%fused_computation.18 | convolution fusion | flops 269484032 | bytes 8388608 | tf_op jit(solution)/shard_map/bmr,bnr->bmn/dot_general | solution.py:194
  261.5 30.3 %gather_fusion.1 = bf16[8192,128]{1,0:T(8,128)(2,1)} fusion(bf16[8192,128]{1,0:T(8,128)(2,1)} %bitcast.162, s32[8192]{0:T(1024)S(1)} %fusion.6), kind=kCustom, calls=%fused_computation.1 | custom fusion | bytes 4227072 | tf_op jit(solution)/shard_map/gather | solution.py:201
  (92 shorter events, 7.8 us)
Async XLA Ops:
  0.0 46.0 %copy-start = (bf16[8192,128]{1,0:T(8,128)(2,1)S(1)}, bf16[8192,128]{1,0:T(8,128)(2,1)}, u32[]{:S(2)}) copy-start(bf16[8192,128]{1,0:T(8,128)(2,1)} %param.11) | copy-start | bytes 6291460
  0.0 15.3 %copy-start.6 = (s32[4]{0:T(128)S(1)}, s32[4]{0:T(128)}, u32[]{:S(2)}) copy-start(s32[4]{0:T(128)} %param.14) | copy-start | bytes 52
  0.0 15.9 %copy-start.4 = (s32[8192]{0:T(1024)S(1)}, s32[8192]{0:T(1024)}, u32[]{:S(2)}) copy-start(s32[8192]{0:T(1024)} %param.10) | copy-start | bytes 98308
  1.9 68.0 %all-to-all-start.1 = ((bf16[128,6,128]{2,1,0:T(8,128)(2,1)}), bf16[128,6,128]{2,1,0:T(8,128)(2,1)S(1)}, u32[]{:S(2)}, u32[]{:S(2)}) async-start(bf16[128,6,128]{2,1,0:T(8,128)(2,1)} %slice.465), calls=%async_computation.1 | async-start | bytes 524288 | tf_op jit(solution)/shard_map/all_to_all | solution.py:169
  51.3 2.4 copy-start.7
  69.9 40.2 %all-to-all-start = ((bf16[128,64,128]{2,1,0:T(8,128)(2,1)}), bf16[128,64,128]{2,1,0:T(8,128)(2,1)S(1)}, u32[]{:S(2)}, u32[]{:S(2)}) async-start(bf16[128,64,128]{2,1,0:T(8,128)(2,1)} %shard_map.91), calls=%async_computation | async-start | bytes 4194304 | tf_op jit(solution)/shard_map/all_to_all | solution.py:168
  110.1 1.3 copy-start.2
  127.0 47.4 %collective-permute-start = (bf16[128,64,128]{2,1,0:T(8,128)(2,1)}, bf16[128,64,128]{2,1,0:T(8,128)(2,1)S(1)}, u32[]{:S(2)}, u32[]{:S(2)}) collective-permute-start(bf16[128,64,128]{2,1,0:T(8,128)(2,1)} %shard_map.92), channel_id=1, source_target_pairs={{0,8},{1,9},{2,10},{3,11},{4,12},{5,13},{6,14},{7,15},{8,0},{9,1},... | collective-permute-start | bytes 6291464 | tf_op jit(solution)/shard_map/ppermute | solution.py:85
  176.9 2.5 copy-start.5
  178.4 48.2 %collective-permute-start.1 = (bf16[128,64,128]{0,2,1:T(8,128)(2,1)}, bf16[128,64,128]{0,2,1:T(8,128)(2,1)}, u32[]{:S(2)}, u32[]{:S(2)}) collective-permute-start(bf16[128,64,128]{0,2,1:T(8,128)(2,1)} %pad_maximum_fusion.1), channel_id=1, source_target_pairs={{0,64},{16,80},{32,96},{48,112},{64,0},{80,16},{96,32},{112,48},{1... | collective-permute-start | bytes 6291464 | tf_op jit(solution)/shard_map/ppermute | solution.py:85
  248.1 6.9 %copy-start.3 = (bf16[8192,128]{1,0:T(8,128)(2,1)S(1)}, bf16[8192,128]{1,0:T(8,128)(2,1)}, u32[]{:S(2)}) copy-start(bf16[8192,128]{1,0:T(8,128)(2,1)} %param.15) | copy-start | bytes 6291460
  261.5 30.3 %copy-start.1 = (bf16[8192,128]{1,0:T(8,128)(2,1)S(1)}, bf16[8192,128]{1,0:T(8,128)(2,1)}, u32[]{:S(2)}) copy-start(bf16[8192,128]{1,0:T(8,128)(2,1)} %param.11) | copy-start | bytes 6291460
